TPU v7x, 32 devices: a whole 2x2x4 slice. The times are simulated.
32 devices in a mesh: net: 4 (over y, x), line: 8 (over z, core).
Axes of the slice: x: 2, y: 2, z: 4, core: 2. Of those that a mesh axis runs over, the one named last changes fastest.
Arguments:
- conductance_inverse: float32 [4, 4096, 4096], P('net', 'line'), may hold values from -0.5 to 4.5, as said below
- prior_voltage: float32 [4, 96, 4096], P('net', None, 'line'), may hold values from -6 to 6
- sources: float32 [3, 4, 4096], P(None, 'net', 'line'), may hold values from -6 to 6
- fault_node: int32 [96], replicated, may hold values from 0 to 16383
- fault_conductance: float32 [96], replicated, may hold values from 0.5 to 4
- terminal_node: int32 [4, 3, 4096], P('net', None, 'line'), may hold values from 0 to 4095
- ownership: int32 [4, 4096], P('net', 'line'), may hold values from 0 to 1, as said below
- partner: int32 [4, 4096], P('net', 'line'), may hold values from 0 to 31, as said below
- delay_steps: int32 [4, 4096], P('net', 'line'), may hold values from 1 to 4, as said below
- surge_conductance: float32 [4, 4096], P('net', 'line'), may hold values from 0.2 to 1
- pole_wave: float32 [4, 6, 4096], P('net', None, 'line'), may hold values from 0.2 to 0.95
- residue_wave: float32 [4, 6, 3, 3, 4096], P('net', None, None, None, 'line'), may hold values from -1 to 1
- pole_admit: float32 [4, 6, 4096], P('net', None, 'line'), may hold values from 0.2 to 0.95
- residue_admit: float32 [4, 6, 3, 3, 4096], P('net', None, None, None, 'line'), may hold values from -1 to 1
- wave_state: float32 [4, 6, 3, 96, 4096], P('net', None, None, None, 'line'), may hold values from -4 to 4
- admit_state: float32 [4, 6, 3, 96, 4096], P('net', None, None, None, 'line'), may hold values from -4 to 4
- wave_history: float32 [4, 4, 3, 96, 4096], P('net', None, None, None, 'line'), may hold values from -6 to 6
Outputs:
- final_voltage: float32 [4, 96, 4096], P('net', None, 'line')
- end_current: float32 [4, 3, 96, 4096], P('net', None, None, 'line')
Inputs may be any that keep to these rules, and one draw needn't show every extreme that they name: `conductance_inverse`: each block is exactly symmetric. `ownership`: A slot is live exactly when the slot of the same number j % 512 at its partner owner is live; the number of live slots differs from owner to owner. The far end of slot j lies in the slot of the same number j % 512 at the partner owner, the partner of that slot is the first owner again, never the owner itself, and at most 17 live slots of one owner have the same partner; this many occur. `delay_steps`: equal at both ends of a line.
All inputs are finite; a program needn't handle non-finite values.
Results may differ from a plain program's by a relative error of at most 0.0003.
Values sent between devices are 32-bit elements; how exact they have to be, the bound alone decides.
A program may use at most 128 MiB of HBM per device.

v0:
```python
import jax
import jax.numpy as jnp
from jax import lax
from jax.sharding import PartitionSpec as P

STEPS = 3


def mix_residue(residue, vector):
    return (
        residue[:, :, 0, None, :] * vector[0]
        + residue[:, :, 1, None, :] * vector[1]
        + residue[:, :, 2, None, :] * vector[2]
    )


def select_delayed(buffer, delay_local):
    depth_count = buffer.shape[0]
    chosen = delay_local[None, :] == jnp.arange(1, depth_count + 1, dtype=jnp.int32)[:, None]
    return jnp.sum(jnp.where(chosen[:, None, None, :], buffer, 0.0), axis=0)


def terminal_values(voltage, terminal):
    picked = jnp.take(voltage, terminal.reshape(-1), axis=1)
    return jnp.moveaxis(picked.reshape(voltage.shape[0], 3, -1), 0, 1)


def spread_ends(history, terminal, node_count):
    values = jnp.moveaxis(history, 0, 1).reshape(history.shape[1], -1)
    return (
        jnp.zeros((history.shape[1], node_count), jnp.float32)
        .at[:, terminal.reshape(-1)]
        .add(values)
    )


def gather_full(block):
    return lax.all_gather(block, "line", axis=1, tiled=True)


def on_device(
    conductance_inverse,
    prior_voltage,
    sources,
    fault_node,
    fault_conductance,
    terminal_node,
    ownership,
    partner,
    delay_steps,
    surge_conductance,
    pole_wave,
    residue_wave,
    pole_admit,
    residue_admit,
    wave_state,
    admit_state,
    wave_history,
):
    inverse_block = conductance_inverse[0]
    row_count = inverse_block.shape[0]
    node_count = inverse_block.shape[1]
    line_index = lax.axis_index("line")
    net_index = lax.axis_index("net")
    offset = line_index * row_count
    net_count = lax.axis_size("net")
    line_count = lax.axis_size("line")
    devices = net_count * line_count
    slot_count = ownership.shape[1]
    capacity = (slot_count + devices - 2) // (devices - 1)
    is_live = ownership[0] > 0
    live_float = is_live.astype(jnp.float32)
    terminal = terminal_node[0]
    delay_local = delay_steps[0]
    surge_local = surge_conductance[0]
    partners = partner[0]
    slot_range = jnp.arange(slot_count, dtype=jnp.int32)
    earlier = (
        (partners[:, None] == partners[None, :])
        & is_live[None, :]
        & (slot_range[None, :] < slot_range[:, None])
    )
    slot_rank = jnp.sum(earlier.astype(jnp.int32), axis=1)
    position = jnp.where(is_live, partners * capacity + slot_rank, devices * capacity)
    scenario_range = jnp.arange(prior_voltage.shape[1], dtype=jnp.int32)
    fault_sub = fault_node // node_count
    fault_local = fault_node % node_count
    fault_here = (fault_sub == net_index) & (fault_local // row_count == line_index)
    wave_decay = pole_wave[0][:, None, None, :]
    admit_decay = pole_admit[0][:, None, None, :]
    wave_res = residue_wave[0]
    admit_res = residue_admit[0]
    voltage = gather_full(prior_voltage[0])
    voltage_rows = prior_voltage[0]
    wave_now = wave_state[0]
    admits = admit_state[0]
    history_buffer = wave_history[0]
    outgoing = None
    current = None
    for step_index in range(STEPS):
        terminal_prior = terminal_values(voltage, terminal)
        admits = admit_decay * admits + mix_residue(admit_res, terminal_prior)
        if step_index == 0:
            wave_now = wave_decay * wave_now + mix_residue(
                wave_res, select_delayed(history_buffer, delay_local)
            )
        else:
            shifted = jnp.concatenate(
                [jnp.zeros_like(history_buffer[:1]), history_buffer[:-1]], axis=0
            )
            wave_now = wave_decay * wave_now + mix_residue(
                wave_res, select_delayed(shifted, delay_local)
            )
            row_width = outgoing.shape[0] * outgoing.shape[1]
            packed = jnp.moveaxis(outgoing, 2, 0).reshape(slot_count, row_width)
            buffer = (
                jnp.zeros((devices * capacity, row_width), jnp.float32)
                .at[position]
                .set(packed, mode="drop")
            )
            arrived = lax.all_to_all(
                buffer, ("net", "line"), split_axis=0, concat_axis=0, tiled=True
            )
            picked_rows = arrived[jnp.minimum(position, devices * capacity - 1)]
            arrived = jnp.moveaxis(picked_rows.reshape(slot_count, 3, -1), 0, 2) * live_float
            newest = jnp.where((delay_local == 1)[None, None, :], arrived, 0.0)
            wave_now = wave_now + mix_residue(wave_res, newest)
            history_buffer = jnp.concatenate([arrived[None], shifted[1:]], axis=0)
        history = (jnp.sum(wave_now, axis=0) - jnp.sum(admits, axis=0)) * live_float
        injection = spread_ends(history, terminal, node_count)
        own_part = (
            lax.dynamic_slice_in_dim(injection, offset, row_count, 1)
            + sources[step_index, 0][None, :]
        )
        injection = lax.dynamic_update_slice_in_dim(injection, own_part, offset, 1)
        fault_value = voltage[scenario_range, fault_local]
        injection = injection.at[scenario_range, fault_local].add(
            jnp.where(fault_here, -fault_conductance * fault_value, 0.0)
        )
        summed = lax.psum(injection, "line")
        voltage_rows = lax.dot_general(
            summed,
            inverse_block,
            (((1,), (1,)), ((), ())),
            precision=lax.Precision.HIGHEST,
            preferred_element_type=jnp.float32,
        )
        voltage = gather_full(voltage_rows)
        terminal_now = terminal_values(voltage, terminal)
        if step_index + 1 < STEPS:
            outgoing = (2.0 * surge_local * terminal_now - history) * live_float
        else:
            current = (surge_local * terminal_now - history) * live_float
    return (voltage_rows[None], current[None])


def solution(mesh):
    return jax.shard_map(
        on_device,
        mesh=mesh,
        in_specs=(
            P("net", "line", None),
            P("net", None, "line"),
            P(None, "net", "line"),
            P(),
            P(),
            P("net", None, "line"),
            P("net", "line"),
            P("net", "line"),
            P("net", "line"),
            P("net", "line"),
            P("net", None, "line"),
            P("net", None, None, None, "line"),
            P("net", None, "line"),
            P("net", None, None, None, "line"),
            P("net", None, None, None, "line"),
            P("net", None, None, None, "line"),
            P("net", None, None, None, "line"),
        ),
        out_specs=(P("net", None, "line"), P("net", None, None, "line")),
        check_vma=False,
    )
```

profile of v0, /device:TPU:0, one launch (start us, length us, event | category | flops | bytes accessed | tf_op | source)
XLA Modules:
  0.0 577.8 jit_solution(13432879487147559588)
XLA Ops:
  7.2 1.9 copy.69
  23.6 2.1 fusion.10
  31.0 1.9 fusion.12
  32.9 8.7 %all-gather.12.cloned.1.call-done = f32[1,96,4096]{1,2,0:T(8,128)} async-done(((f32[1,96,512]{1,2,0:T(8,128)}), f32[1,96,4096]{1,2,0:T(8,128)}) %all-gather.12.cloned.1.call-update) | async-done | bytes 1572880 | tf_op jit(solution)/shard_map/all_gather | solution.py:38
  41.5 3.6 gather_fusion
  45.1 5.6 gather_fusion.5
  53.1 1.8 copy.70
  54.9 1.8 copy.72
  56.6 1.8 copy.71
  58.4 2.4 fusion.31
  62.5 2.2 copy.74
  64.7 10.5 %scatter_custom_fusion = f32[96,4096]{0,1:T(8,128)} fusion(s32[1536]{0:T(1024)} %fusion.32, f32[1536,96]{1,0:T(8,128)} %copy.74, f32[]{:T(128)} %constant.37.clone.1), kind=kCustom, calls=%fused_computation.47 | custom fusion | flops 147456 | bytes 1573376 | tf_op jit(solution)/shard_map/scatter-add | solution.py:33
  75.3 1.8 add_dynamic-update-slice_fusion.2
  77.0 2.8 copy.75
  81.1 12.2 %scatter_fusion = f32[96,4096]{1,0:T(8,128)} fusion(f32[96,4096]{1,0:T(8,128)} %copy.75, s32[96]{0:T(128)S(1)} %fusion.36, f32[96]{0:T(128)} %get-tuple-element.9), kind=kCustom, calls=%fused_computation.10 | custom fusion | flops 96 | bytes 1920 | tf_op jit(solution)/shard_map/scatter-add | solution.py:137
  93.6 61.2 %all-reduce.6.cloned.1.call-done = f32[96,4096]{1,0:T(8,128)} async-done(((f32[96,4096]{1,0:T(8,128)}), f32[96,4096]{1,0:T(8,128)}) %all-reduce.6.cloned.1.call-update) | async-done | bytes 1572880 | tf_op jit(solution)/shard_map/psum | solution.py:140
  154.8 12.7 %fusion.4 = f32[96,512]{1,0:T(8,128)} fusion(f32[96,4096]{1,0:T(8,128)} %all-reduce.6.cloned.1.call-done, f32[1,512,4096]{2,1,0:T(8,128)} %param.19), kind=kOutput, calls=%fused_computation.21 | convolution fusion | flops 2415919104 | bytes 10158080 | tf_op jit(solution)/shard_map/dot_general | solution.py:141
  171.6 2.8 slice_bitcast_fusion
  174.4 17.7 %all-gather.6.cloned.1.call-done = f32[96,4096]{1,0:T(8,128)} async-done(((f32[96,512]{1,0:T(8,128)}), f32[96,4096]{1,0:T(8,128)}) %all-gather.6.cloned.1.call-update) | async-done | bytes 1572880 | tf_op jit(solution)/shard_map/all_gather | solution.py:38
  192.1 2.8 copy.76
  194.9 5.6 gather_fusion.6
  200.5 2.3 broadcast_select_fusion.2
  202.8 2.2 copy.77
  205.0 2.4 fusion.23
  207.4 2.2 copy.78
  209.6 3.7 scatter_custom_fusion.2
  213.4 2.3 all_to_all.16
  215.7 3.8 all-to-all-start
  222.3 2.0 slice_bitcast_fusion.6
  224.3 1.8 copy.80
  226.0 1.7 copy.82
  227.8 1.8 copy.81
  229.6 3.5 gather_fusion.2
  234.3 4.2 fusion.11
  238.5 11.3 %all-to-all-done = f32[32,17,288]{2,1,0:T(8,128)} async-done(((f32[32,17,288]{2,1,0:T(8,128)}), f32[32,17,288]{2,1,0:T(8,128)}, u32[]{:S(2)}, u32[]{:S(2)}) %all-to-all-start) | async-done | bytes 626720 | tf_op jit(solution)/shard_map/all_to_all | solution.py:121
  256.8 3.9 fusion.38
  262.1 9.4 %scatter_custom_fusion.3 = f32[96,4096]{0,1:T(8,128)S(1)} fusion(s32[1536]{0:T(1024)} %fusion.32, f32[1536,96]{1,0:T(8,128)S(1)} %copy.84, f32[]{:T(128)} %constant.37.clone.1), kind=kCustom, calls=%fused_computation.45 | custom fusion | flops 147456 | bytes 1573376 | tf_op jit(solution)/shard_map/scatter-add | solution.py:33
  271.6 1.7 copy.85
  273.3 12.2 %scatter_fusion.1 = f32[96,4096]{1,0:T(8,128)} fusion(f32[96,4096]{1,0:T(8,128)} %copy.85, s32[96]{0:T(128)S(1)} %fusion.36, f32[96]{0:T(128)S(1)} %copy-done.45), kind=kCustom, calls=%fused_computation.13 | custom fusion | flops 96 | bytes 1920 | tf_op jit(solution)/shard_map/scatter-add | solution.py:137
  286.0 59.3 %all-reduce.8.cloned.1.call-done = f32[96,4096]{1,0:T(8,128)} async-done(((f32[96,4096]{1,0:T(8,128)}), f32[96,4096]{1,0:T(8,128)}) %all-reduce.8.cloned.1.call-update) | async-done | bytes 1572880 | tf_op jit(solution)/shard_map/psum | solution.py:140
  345.3 12.6 %fusion.2 = f32[96,512]{1,0:T(8,128)} fusion(f32[96,4096]{1,0:T(8,128)} %all-reduce.8.cloned.1.call-done, f32[1,512,4096]{2,1,0:T(8,128)} %param.19), kind=kOutput, calls=%fused_computation.19 | convolution fusion | flops 2415919104 | bytes 10158080 | tf_op jit(solution)/shard_map/dot_general | solution.py:141
  358.8 23.8 %all-gather.8.cloned.1.call-done = f32[96,4096]{1,0:T(8,128)} async-done(((f32[96,512]{1,0:T(8,128)}), f32[96,4096]{1,0:T(8,128)}) %all-gather.8.cloned.1.call-update) | async-done | bytes 1572880 | tf_op jit(solution)/shard_map/all_gather | solution.py:38
  382.6 1.8 copy.86
  384.5 3.7 gather_fusion.7
  390.5 3.3 scatter_custom_fusion.5
  393.8 2.5 all_to_all.19
  396.3 3.8 all-to-all-start.1
  400.3 2.0 slice_bitcast_fusion.3
  402.4 1.7 copy.90
  404.1 1.8 copy.92
  405.9 1.8 copy.91
  407.6 3.5 gather_fusion.4
  412.3 4.8 add_reduce_fusion
  417.2 13.2 %all-to-all-done.1 = f32[32,17,288]{2,1,0:T(8,128)} async-done(((f32[32,17,288]{2,1,0:T(8,128)}), f32[32,17,288]{2,1,0:T(8,128)}, u32[]{:S(2)}, u32[]{:S(2)}) %all-to-all-start.1) | async-done | bytes 626720 | tf_op jit(solution)/shard_map/all_to_all | solution.py:121
  431.8 2.4 gather_fusion.3
  434.2 2.3 copy.89
  437.8 3.1 add_reduce_fusion.1
  442.0 9.4 %scatter_custom_fusion.6 = f32[96,4096]{0,1:T(8,128)S(1)} fusion(s32[1536]{0:T(1024)} %fusion.32, f32[1536,96]{1,0:T(8,128)S(1)} %copy.94, f32[]{:T(128)} %constant.37.clone.1), kind=kCustom, calls=%fused_computation.43 | custom fusion | flops 147456 | bytes 1573376 | tf_op jit(solution)/shard_map/scatter-add | solution.py:33
  453.2 12.2 %scatter_fusion.2 = f32[96,4096]{1,0:T(8,128)} fusion(f32[96,4096]{1,0:T(8,128)} %copy.95, s32[96]{0:T(128)S(1)} %fusion.36, f32[96]{0:T(128)S(1)} %copy-done.44), kind=kCustom, calls=%fused_computation.16 | custom fusion | flops 96 | bytes 1920 | tf_op jit(solution)/shard_map/scatter-add | solution.py:137
  465.7 59.5 %all-reduce.10.cloned.1.call-done = f32[96,4096]{1,0:T(8,128)} async-done(((f32[96,4096]{1,0:T(8,128)}), f32[96,4096]{1,0:T(8,128)}) %all-reduce.10.cloned.1.call-update) | async-done | bytes 1572880 | tf_op jit(solution)/shard_map/psum | solution.py:140
  525.2 12.7 %fusion = f32[96,512]{1,0:T(8,128)} fusion(f32[96,4096]{1,0:T(8,128)} %all-reduce.10.cloned.1.call-done, f32[1,512,4096]{2,1,0:T(8,128)} %param.19), kind=kOutput, calls=%fused_computation.17 | convolution fusion | flops 2415919104 | bytes 10158080 | tf_op jit(solution)/shard_map/dot_general | solution.py:141
  537.9 24.6 %all-gather.10.cloned.1.call-done = f32[96,4096]{1,0:T(8,128)} async-done(((f32[96,512]{1,0:T(8,128)}), f32[96,4096]{1,0:T(8,128)}) %all-gather.10.cloned.1.call-update) | async-done | bytes 1572880 | tf_op jit(solution)/shard_map/all_gather | solution.py:38
  562.5 1.8 copy.96
  564.4 3.7 gather_fusion.8
  (175 shorter events, 55.1 us)
Async XLA Ops:
  7.2 18.5 %copy-start.46 = (s32[96]{0:T(128)S(1)}, s32[96]{0:T(128)}, u32[]{:S(2)}) copy-start(s32[96]{0:T(128)} %param.22) | copy-start | bytes 1156
  7.2 23.8 %copy-start.2 = (f32[1,6,3,96,512]{4,3,2,1,0:T(8,128)S(1)}, f32[1,6,3,96,512]{4,3,2,1,0:T(8,128)}, u32[]{:S(2)}) copy-start(f32[1,6,3,96,512]{4,3,2,1,0:T(8,128)} %param.33) | copy-start | bytes 10616836
  7.2 34.3 %all-gather.12.cloned.1.call-start = ((), (), s32[]{:S(2)}) async-start(), calls=%async_computation.8 | async-start | bytes 2359296 | tf_op jit(solution)/shard_map/all_gather | solution.py:38
  9.2 145.6 %all-reduce.6.cloned.1.call-start = ((), (), s32[]{:S(2)}) async-start(), calls=%async_computation.2 | async-start | bytes 3145728 | tf_op jit(solution)/shard_map/psum | solution.py:140
  9.9 0.5 copy-start.43
  12.5 11.2 %copy-start.35 = (s32[1536]{0:T(1024)}, s32[1536]{0:T(1024)S(1)}, u32[]{:S(2)}) copy-start(s32[1536]{0:T(1024)S(1)} %reshape_squeeze.5) | copy-start | bytes 18436
  20.2 10.8 %copy-start.25 = (f32[6,3,1,512]{3,1,2,0:T(4,128)S(1)}, f32[6,3,1,512]{3,1,2,0:T(4,128)}, u32[]{:S(2)}) copy-start(f32[6,3,1,512]{3,1,2,0:T(4,128)} %copy.124) | copy-start | bytes 110596
  20.2 10.8 %copy-start.31 = (f32[1,6,512]{2,1,0:T(8,128)S(1)}, f32[1,6,512]{2,1,0:T(8,128)}, u32[]{:S(2)}) copy-start(f32[1,6,512]{2,1,0:T(8,128)} %copy.126) | copy-start | bytes 36868
  23.6 4.2 copy-start.36
  25.7 2.1 copy-start.47
  28.6 1.6 copy-start.27
  28.6 1.6 copy-start.29
  30.2 0.7 copy-start.19
  30.2 0.8 copy-start.21
  30.2 0.8 copy-start.23
  50.7 7.7 %copy-start = (f32[1,6,3,96,512]{4,3,2,1,0:T(8,128)S(1)}, f32[1,6,3,96,512]{4,3,2,1,0:T(8,128)}, u32[]{:S(2)}) copy-start(f32[1,6,3,96,512]{4,3,2,1,0:T(8,128)} %param.34) | copy-start | bytes 10616836
  58.4 2.4 copy-start.9
  60.8 0.8 copy-start.12
  93.4 98.7 %all-gather.6.cloned.1.call-start = ((), (), s32[]{:S(2)}) async-start(), calls=%async_computation.3 | async-start | bytes 1769472 | tf_op jit(solution)/shard_map/all_gather | solution.py:38
  215.7 34.1 %all-to-all-start = ((f32[32,17,288]{2,1,0:T(8,128)}), f32[32,17,288]{2,1,0:T(8,128)}, u32[]{:S(2)}, u32[]{:S(2)}) async-start(f32[32,17,288]{2,1,0:T(8,128)} %all_to_all.16), calls=%async_computation | async-start | bytes 2359296 | tf_op jit(solution)/shard_map/all_to_all | solution.py:121
  219.5 125.8 %all-reduce.8.cloned.1.call-start = ((), (), s32[]{:S(2)}) async-start(), calls=%async_computation.4 | async-start | bytes 3145728 | tf_op jit(solution)/shard_map/psum | solution.py:140
  253.2 0.8 copy-start.13
  253.2 2.3 copy-start.5
  253.2 2.3 copy-start.37
  254.1 2.7 copy-start.3
  254.1 2.7 copy-start.20
  254.1 2.7 copy-start.22
  254.1 2.7 copy-start.24
  254.1 2.7 copy-start.26
  254.1 2.7 copy-start.28
  254.1 2.7 copy-start.30
  254.2 2.7 copy-start.32
  256.8 4.8 copy-start.14
  260.8 0.9 copy-start.10
  260.8 10.7 %copy-start.41 = (f32[1,1,512]{2,1,0:T(1,128)S(1)}, f32[1,1,512]{2,1,0:T(1,128)}, u32[]{:S(2)}) copy-start(f32[1,1,512]{2,1,0:T(1,128)} %get-tuple-element.45) | copy-start | bytes 6148
  261.8 11.6 %copy-start.45 = (f32[96]{0:T(128)S(1)}, f32[96]{0:T(128)}, u32[]{:S(2)}) copy-start(f32[96]{0:T(128)} %multiply_select_fusion.1) | copy-start | bytes 1156
  285.6 72.4 %copy-start.18 = (f32[3,96,512]{2,1,0:T(8,128)S(1)}, f32[3,96,512]{2,1,0:T(8,128)}, u32[]{:S(2)}) copy-start(f32[3,96,512]{2,1,0:T(8,128)} %get-tuple-element.3) | copy-start | bytes 1769476
  285.6 97.0 %all-gather.8.cloned.1.call-start = ((), (), s32[]{:S(2)}) async-start(), calls=%async_computation.5 | async-start | bytes 1769472 | tf_op jit(solution)/shard_map/all_gather | solution.py:38
  358.0 26.5 %copy-start.33 = (s32[2048]{0:T(1024)S(1)}, s32[2048]{0:T(1024)}, u32[]{:S(2)}) copy-start(s32[2048]{0:T(1024)} %pad_clamp_fusion) | copy-start | bytes 24580
  384.4 5.4 copy-start.11
  384.5 5.4 copy-start.15
  384.5 5.4 copy-start.38
  389.6 0.9 copy-start.6
  393.8 18.5 %copy-start.1 = (f32[1,6,3,96,512]{4,3,2,1,0:T(8,128)S(1)}, f32[1,6,3,96,512]{4,3,2,1,0:T(8,128)}, u32[]{:S(2)}) copy-start(f32[1,6,3,96,512]{4,3,2,1,0:T(8,128)} %param.34) | copy-start | bytes 10616836
  396.3 34.1 %all-to-all-start.1 = ((f32[32,17,288]{2,1,0:T(8,128)}), f32[32,17,288]{2,1,0:T(8,128)}, u32[]{:S(2)}, u32[]{:S(2)}) async-start(f32[32,17,288]{2,1,0:T(8,128)} %all_to_all.19), calls=%async_computation.1 | async-start | bytes 2359296 | tf_op jit(solution)/shard_map/all_to_all | solution.py:121
  400.1 125.1 %all-reduce.10.cloned.1.call-start = ((), (), s32[]{:S(2)}) async-start(), calls=%async_computation.6 | async-start | bytes 3145728 | tf_op jit(solution)/shard_map/psum | solution.py:140
  431.8 4.8 copy-start.42
  434.2 3.5 copy-start.4
  437.7 3.1 copy-start.7
  440.8 0.8 copy-start.16
  440.8 10.5 %copy-start.40 = (f32[1,1,512]{2,1,0:T(1,128)S(1)}, f32[1,1,512]{2,1,0:T(1,128)}, u32[]{:S(2)}) copy-start(f32[1,1,512]{2,1,0:T(1,128)} %get-tuple-element.43) | copy-start | bytes 6148
  441.7 11.5 %copy-start.44 = (f32[96]{0:T(128)S(1)}, f32[96]{0:T(128)}, u32[]{:S(2)}) copy-start(f32[96]{0:T(128)} %multiply_select_fusion) | copy-start | bytes 1156
  465.5 97.0 %all-gather.10.cloned.1.call-start = ((), (), s32[]{:S(2)}) async-start(), calls=%async_computation.7 | async-start | bytes 1769472 | tf_op jit(solution)/shard_map/all_gather | solution.py:38
  537.9 26.5 %copy-start.34 = (s32[2048]{0:T(1024)S(1)}, s32[2048]{0:T(1024)}, u32[]{:S(2)}) copy-start(s32[2048]{0:T(1024)} %pad_clamp_fusion) | copy-start | bytes 24580
  564.4 5.4 copy-start.8
  564.4 5.4 copy-start.17
  564.4 5.4 copy-start.39
Sparse Core Ops, SparseCore 0:
  9.6 31.8 all-gather.11
  93.5 61.2 all-reduce.5
  167.6 24.4 all-gather.5
  285.7 59.5 all-reduce.7
  358.1 24.4 all-gather.7
  465.6 59.5 all-reduce.9
  538.0 24.4 all-gather.9
where the time goes:
time: 587 us; the launch traced here: 578 us
  waiting for transfers between devices  279 us (48%)
  other arithmetic  122 us (21%)
  local copies, waits for them, and re-layouts  115 us (20%)
  matrix products  38 us (6%)
  between operations  15.2 us (3%)
  starting transfers between devices  9.15 us (2%)
    psum x3, waiting for transfers between devices, on_device(): summed = lax.psum(injection, 'line')  180 us
    all_gather x4, waiting for transfers between devices, gather_full(): return lax.all_gather(block, 'line', axis=1, tiled=True)  74.8 us
    dot_general x3, matrix products, on_device(): lax.dot_general(summed, inverse_block, (((1,), (1,)), ((), ())), precisio...  38 us
    scatter-add x3, other arithmetic, on_device(): injection.at[scenario_range, fault_local]  36.6 us
    scatter-add x3, other arithmetic, spread_ends(): return jnp.zeros((history.shape[1], node_count), jnp.float32).at[:, termi...  29.3 us
    all_to_all x2, waiting for transfers between devices, on_device(): lax.all_to_all(buffer, ('net', 'line'), split_axis=0, concat_axis=0, tile...  24.6 us
    reduce_sum x6, other arithmetic, on_device(): history = (jnp.sum(wave_now, axis=0) - jnp.sum(admits, axis=0)) * live_float  20.3 us
    gather x4, local copies, waits for them, and re-layouts, terminal_values(): picked = jnp.take(voltage, terminal.reshape(-1), axis=1)  18.5 us
  transfers between devices with their start and end apart: 9, of which 9 were waited for; matrix products, arithmetic and copies ran while one was open for 11% of the time, Pallas kernels for 0%

commit v1 on v0

--- a/solution.py
+++ b/solution.py
@@ -137,7 +137,7 @@
         injection = injection.at[scenario_range, fault_local].add(
             jnp.where(fault_here, -fault_conductance * fault_value, 0.0)
         )
-        summed = lax.psum(injection, "line")
+        summed = jnp.sum(lax.all_gather(injection, "line"), axis=0)
         voltage_rows = lax.dot_general(
             summed,
             inverse_block,

time: 587 us -> 764 us (1.30)
  waiting for transfers between devices: 279 us -> 439 us
  other arithmetic: 122 us -> 139 us
    all_gather x0 -> x3, waiting for transfers between devices: none -> 344 us  [on_device(): summed = jnp.sum(lax.all_gather(injection, 'line'), axis=0)]
    psum x3 -> x0, waiting for transfers between devices: 180 us -> none  [on_device(): summed = lax.psum(injection, 'line')]
    reduce_sum x0 -> x3, other arithmetic: none -> 18.3 us  [on_device(): summed = jnp.sum(lax.all_gather(injection, 'line'), axis=0)]
  transfers between devices with their start and end apart: 9 -> 9, of which waited for: 9 -> 9; matrix products, arithmetic and copies ran while one was open for 11% -> 9% of each run, Pallas kernels for 0% -> 0%
where the time goes in v1:
time: 764 us; the launch traced here: 754 us
  waiting for transfers between devices  439 us (57%)
  other arithmetic  139 us (18%)
  local copies, waits for them, and re-layouts  116 us (15%)
  matrix products  35 us (5%)
  between operations  15.1 us (2%)
  starting transfers between devices  9.15 us (1%)
    all_gather x3, waiting for transfers between devices, on_device(): summed = jnp.sum(lax.all_gather(injection, 'line'), axis=0)  344 us
    all_gather x4, waiting for transfers between devices, gather_full(): return lax.all_gather(block, 'line', axis=1, tiled=True)  70.4 us
    scatter-add x3, other arithmetic, on_device(): injection.at[scenario_range, fault_local]  36.7 us
    dot_general x3, matrix products, on_device(): lax.dot_general(summed, inverse_block, (((1,), (1,)), ((), ())), precisio...  35 us
    scatter-add x3, other arithmetic, spread_ends(): return jnp.zeros((history.shape[1], node_count), jnp.float32).at[:, termi...  29.5 us
    all_to_all x2, waiting for transfers between devices, on_device(): lax.all_to_all(buffer, ('net', 'line'), split_axis=0, concat_axis=0, tile...  24.3 us
    reduce_sum x6, other arithmetic, on_device(): history = (jnp.sum(wave_now, axis=0) - jnp.sum(admits, axis=0)) * live_float  20.3 us
    gather x4, local copies, waits for them, and re-layouts, terminal_values(): picked = jnp.take(voltage, terminal.reshape(-1), axis=1)  18.6 us
  transfers between devices with their start and end apart: 9, of which 9 were waited for; matrix products, arithmetic and copies ran while one was open for 9% of the time, Pallas kernels for 0%

profile of v1, /device:TPU:0, one launch (start us, length us, event | category | flops | bytes accessed | tf_op | source)
XLA Modules:
  0.0 753.8 jit_solution(11891334055179664168)
XLA Ops:
  7.2 1.9 copy.69
  23.7 2.1 fusion.10
  31.0 1.9 fusion.12
  32.9 8.6 %all-gather.18.cloned.1.call-done = f32[1,96,4096]{1,2,0:T(8,128)} async-done(((f32[1,96,512]{1,2,0:T(8,128)}), f32[1,96,4096]{1,2,0:T(8,128)}) %all-gather.18.cloned.1.call-update) | async-done | bytes 1572880 | tf_op jit(solution)/shard_map/all_gather | solution.py:38
  41.5 3.6 gather_fusion
  45.1 5.6 gather_fusion.5
  54.9 1.8 copy.72
  56.6 1.8 copy.71
  58.4 2.4 fusion.31
  62.5 2.2 copy.74
  64.7 10.5 %scatter_custom_fusion = f32[96,4096]{0,1:T(8,128)} fusion(s32[1536]{0:T(1024)} %fusion.32, f32[1536,96]{1,0:T(8,128)} %copy.74, f32[]{:T(128)} %constant.37.clone.1), kind=kCustom, calls=%fused_computation.47 | custom fusion | flops 147456 | bytes 1573376 | tf_op jit(solution)/shard_map/scatter-add | solution.py:33
  75.3 1.8 add_dynamic-update-slice_fusion.2
  77.0 2.8 copy.75
  81.1 12.3 %scatter_fusion = f32[96,4096]{1,0:T(8,128)} fusion(f32[96,4096]{1,0:T(8,128)} %copy.75, s32[96]{0:T(128)S(1)} %fusion.36, f32[96]{0:T(128)} %get-tuple-element.9), kind=kCustom, calls=%fused_computation.10 | custom fusion | flops 96 | bytes 1920 | tf_op jit(solution)/shard_map/scatter-add | solution.py:137
  93.6 116.0 %all-gather.20.cloned.1.call-done = f32[768,4096]{1,0:T(8,128)} async-done(((f32[96,4096]{1,0:T(8,128)}), f32[768,4096]{1,0:T(8,128)}) %all-gather.20.cloned.1.call-update) | async-done | bytes 12582928 | tf_op jit(solution)/shard_map/all_gather | solution.py:140
  209.7 6.9 reduce_sum.125
  216.5 12.7 %fusion.4 = f32[96,512]{1,0:T(8,128)} fusion(f32[96,4096]{1,0:T(8,128)} %reduce_sum.125, f32[1,512,4096]{2,1,0:T(8,128)} %param.19), kind=kOutput, calls=%fused_computation.21 | convolution fusion | flops 2415919104 | bytes 10158080 | tf_op jit(solution)/shard_map/dot_general | solution.py:141
  233.4 2.9 slice_bitcast_fusion
  236.2 16.6 %all-gather.12.cloned.1.call-done = f32[96,4096]{1,0:T(8,128)} async-done(((f32[96,512]{1,0:T(8,128)}), f32[96,4096]{1,0:T(8,128)}) %all-gather.12.cloned.1.call-update) | async-done | bytes 1572880 | tf_op jit(solution)/shard_map/all_gather | solution.py:38
  252.8 2.8 copy.76
  255.6 5.6 gather_fusion.6
  261.2 2.3 broadcast_select_fusion.2
  263.5 2.2 copy.77
  265.7 2.4 fusion.23
  268.2 2.2 copy.78
  270.4 3.7 scatter_custom_fusion.2
  274.1 2.3 all_to_all.16
  276.4 3.8 all-to-all-start
  283.0 2.0 slice_bitcast_fusion.6
  285.0 1.8 copy.80
  286.8 1.8 copy.82
  290.3 3.5 gather_fusion.2
  295.1 4.2 fusion.11
  299.3 11.3 %all-to-all-done = f32[32,17,288]{2,1,0:T(8,128)} async-done(((f32[32,17,288]{2,1,0:T(8,128)}), f32[32,17,288]{2,1,0:T(8,128)}, u32[]{:S(2)}, u32[]{:S(2)}) %all-to-all-start) | async-done | bytes 626720 | tf_op jit(solution)/shard_map/all_to_all | solution.py:121
  316.5 3.9 fusion.38
  321.7 9.6 %scatter_custom_fusion.3 = f32[96,4096]{0,1:T(8,128)S(1)} fusion(s32[1536]{0:T(1024)} %fusion.32, f32[1536,96]{1,0:T(8,128)} %copy.84, f32[]{:T(128)} %constant.37.clone.1), kind=kCustom, calls=%fused_computation.45 | custom fusion | flops 147456 | bytes 1573376 | tf_op jit(solution)/shard_map/scatter-add | solution.py:33
  333.3 12.2 %scatter_fusion.1 = f32[96,4096]{1,0:T(8,128)} fusion(f32[96,4096]{1,0:T(8,128)} %copy.85, s32[96]{0:T(128)S(1)} %fusion.36, f32[96]{0:T(128)S(1)} %copy-done.41), kind=kCustom, calls=%fused_computation.13 | custom fusion | flops 96 | bytes 1920 | tf_op jit(solution)/shard_map/scatter-add | solution.py:137
  346.0 114.1 %all-gather.22.cloned.1.call-done = f32[768,4096]{1,0:T(8,128)} async-done(((f32[96,4096]{1,0:T(8,128)}), f32[768,4096]{1,0:T(8,128)}) %all-gather.22.cloned.1.call-update) | async-done | bytes 12582928 | tf_op jit(solution)/shard_map/all_gather | solution.py:140
  460.1 5.7 reduce_sum.129
  465.8 11.2 %fusion.2 = f32[96,512]{1,0:T(8,128)} fusion(f32[96,4096]{1,0:T(8,128)S(1)} %reduce_sum.129, f32[1,512,4096]{2,1,0:T(8,128)} %param.19), kind=kOutput, calls=%fused_computation.19 | convolution fusion | flops 2415919104 | bytes 10158080 | tf_op jit(solution)/shard_map/dot_general | solution.py:141
  477.0 2.0 slice_bitcast_fusion.15
  479.0 21.6 %all-gather.14.cloned.1.call-done = f32[96,4096]{1,0:T(8,128)} async-done(((f32[96,512]{1,0:T(8,128)}), f32[96,4096]{1,0:T(8,128)}) %all-gather.14.cloned.1.call-update) | async-done | bytes 1572880 | tf_op jit(solution)/shard_map/all_gather | solution.py:38
  500.6 1.8 copy.86
  502.5 3.7 gather_fusion.7
  508.5 3.3 scatter_custom_fusion.5
  511.7 2.4 all_to_all.19
  514.2 3.8 all-to-all-start.1
  518.3 2.0 slice_bitcast_fusion.3
  520.3 1.8 copy.90
  522.0 1.8 copy.92
  525.5 3.6 gather_fusion.4
  530.4 4.8 add_reduce_fusion
  535.2 13.1 %all-to-all-done.1 = f32[32,17,288]{2,1,0:T(8,128)} async-done(((f32[32,17,288]{2,1,0:T(8,128)}), f32[32,17,288]{2,1,0:T(8,128)}, u32[]{:S(2)}, u32[]{:S(2)}) %all-to-all-start.1) | async-done | bytes 626720 | tf_op jit(solution)/shard_map/all_to_all | solution.py:121
  549.7 2.3 gather_fusion.3
  552.0 2.3 copy.89
  555.5 3.1 add_reduce_fusion.1
  559.8 9.4 %scatter_custom_fusion.6 = f32[96,4096]{0,1:T(8,128)S(1)} fusion(s32[1536]{0:T(1024)} %fusion.32, f32[1536,96]{1,0:T(8,128)S(1)} %copy.94, f32[]{:T(128)} %constant.37.clone.1), kind=kCustom, calls=%fused_computation.43 | custom fusion | flops 147456 | bytes 1573376 | tf_op jit(solution)/shard_map/scatter-add | solution.py:33
  571.0 12.3 %scatter_fusion.2 = f32[96,4096]{1,0:T(8,128)} fusion(f32[96,4096]{1,0:T(8,128)} %copy.95, s32[96]{0:T(128)S(1)} %fusion.36, f32[96]{0:T(128)S(1)} %copy-done.40), kind=kCustom, calls=%fused_computation.16 | custom fusion | flops 96 | bytes 1920 | tf_op jit(solution)/shard_map/scatter-add | solution.py:137
  583.6 114.3 %all-gather.24.cloned.1.call-done = f32[768,4096]{1,0:T(8,128)} async-done(((f32[96,4096]{1,0:T(8,128)}), f32[768,4096]{1,0:T(8,128)}) %all-gather.24.cloned.1.call-update) | async-done | bytes 12582928 | tf_op jit(solution)/shard_map/all_gather | solution.py:140
  697.9 5.7 reduce_sum.132
  703.6 11.2 %fusion = f32[96,512]{1,0:T(8,128)} fusion(f32[96,4096]{1,0:T(8,128)S(1)} %reduce_sum.132, f32[1,512,4096]{2,1,0:T(8,128)} %param.19), kind=kOutput, calls=%fused_computation.17 | convolution fusion | flops 2415919104 | bytes 10158080 | tf_op jit(solution)/shard_map/dot_general | solution.py:141
  714.8 23.6 %all-gather.16.cloned.1.call-done = f32[96,4096]{1,0:T(8,128)} async-done(((f32[96,512]{1,0:T(8,128)}), f32[96,4096]{1,0:T(8,128)}) %all-gather.16.cloned.1.call-update) | async-done | bytes 1572880 | tf_op jit(solution)/shard_map/all_gather | solution.py:38
  738.4 1.8 copy.96
  740.3 3.7 gather_fusion.8
  (170 shorter events, 60.4 us)
Async XLA Ops:
  7.2 18.6 %copy-start.42 = (s32[96]{0:T(128)S(1)}, s32[96]{0:T(128)}, u32[]{:S(2)}) copy-start(s32[96]{0:T(128)} %param.22) | copy-start | bytes 1156
  7.2 23.9 %copy-start.2 = (f32[1,6,3,96,512]{4,3,2,1,0:T(8,128)S(1)}, f32[1,6,3,96,512]{4,3,2,1,0:T(8,128)}, u32[]{:S(2)}) copy-start(f32[1,6,3,96,512]{4,3,2,1,0:T(8,128)} %param.33) | copy-start | bytes 10616836
  7.2 34.3 %all-gather.18.cloned.1.call-start = ((), (), s32[]{:S(2)}) async-start(), calls=%async_computation.5 | async-start | bytes 2359296 | tf_op jit(solution)/shard_map/all_gather | solution.py:38
  9.2 200.5 %all-gather.20.cloned.1.call-start = ((), (), s32[]{:S(2)}) async-start(), calls=%async_computation.6 | async-start | bytes 14155776 | tf_op jit(solution)/shard_map/all_gather | solution.py:140
  9.9 0.6 copy-start.39
  12.5 11.2 %copy-start.30 = (s32[1536]{0:T(1024)}, s32[1536]{0:T(1024)S(1)}, u32[]{:S(2)}) copy-start(s32[1536]{0:T(1024)S(1)} %reshape_squeeze.5) | copy-start | bytes 18436
  20.3 10.7 %copy-start.20 = (f32[6,3,1,512]{3,1,2,0:T(4,128)S(1)}, f32[6,3,1,512]{3,1,2,0:T(4,128)}, u32[]{:S(2)}) copy-start(f32[6,3,1,512]{3,1,2,0:T(4,128)} %copy.124) | copy-start | bytes 110596
  20.3 10.7 %copy-start.26 = (f32[1,6,512]{2,1,0:T(8,128)S(1)}, f32[1,6,512]{2,1,0:T(8,128)}, u32[]{:S(2)}) copy-start(f32[1,6,512]{2,1,0:T(8,128)} %copy.126) | copy-start | bytes 36868
  23.7 4.1 copy-start.31
  25.8 2.0 copy-start.43
  28.7 1.6 copy-start.22
  28.7 1.6 copy-start.24
  30.2 0.7 copy-start.14
  30.2 0.7 copy-start.16
  30.2 0.8 copy-start.18
  50.7 7.7 %copy-start = (f32[1,6,3,96,512]{4,3,2,1,0:T(8,128)S(1)}, f32[1,6,3,96,512]{4,3,2,1,0:T(8,128)}, u32[]{:S(2)}) copy-start(f32[1,6,3,96,512]{4,3,2,1,0:T(8,128)} %param.34) | copy-start | bytes 10616836
  58.4 2.4 copy-start.9
  60.8 0.8 copy-start.10
  93.4 159.4 %all-gather.12.cloned.1.call-start = ((), (), s32[]{:S(2)}) async-start(), calls=%async_computation.2 | async-start | bytes 1769472 | tf_op jit(solution)/shard_map/all_gather | solution.py:38
  276.4 34.1 %all-to-all-start = ((f32[32,17,288]{2,1,0:T(8,128)}), f32[32,17,288]{2,1,0:T(8,128)}, u32[]{:S(2)}, u32[]{:S(2)}) async-start(f32[32,17,288]{2,1,0:T(8,128)} %all_to_all.16), calls=%async_computation | async-start | bytes 2359296 | tf_op jit(solution)/shard_map/all_to_all | solution.py:121
  280.3 179.8 %all-gather.22.cloned.1.call-start = ((), (), s32[]{:S(2)}) async-start(), calls=%async_computation.7 | async-start | bytes 14155776 | tf_op jit(solution)/shard_map/all_gather | solution.py:140
  311.9 2.1 copy-start.38
  313.7 1.5 copy-start.5
  313.7 1.5 copy-start.32
  314.0 2.4 copy-start.3
  314.1 2.3 copy-start.15
  314.1 2.3 copy-start.17
  314.1 2.3 copy-start.19
  314.1 2.3 copy-start.21
  314.1 2.3 copy-start.23
  314.1 2.3 copy-start.25
  314.1 2.3 copy-start.27
  316.5 3.9 copy-start.11
  320.4 11.0 %copy-start.37 = (f32[1,1,512]{2,1,0:T(1,128)S(1)}, f32[1,1,512]{2,1,0:T(1,128)}, u32[]{:S(2)}) copy-start(f32[1,1,512]{2,1,0:T(1,128)} %get-tuple-element.45) | copy-start | bytes 6148
  320.6 12.7 %copy-start.41 = (f32[96]{0:T(128)S(1)}, f32[96]{0:T(128)}, u32[]{:S(2)}) copy-start(f32[96]{0:T(128)} %multiply_select_fusion.1) | copy-start | bytes 1156
  345.5 155.1 %all-gather.14.cloned.1.call-start = ((), (), s32[]{:S(2)}) async-start(), calls=%async_computation.3 | async-start | bytes 1769472 | tf_op jit(solution)/shard_map/all_gather | solution.py:38
  477.0 25.5 %copy-start.28 = (s32[2048]{0:T(1024)S(1)}, s32[2048]{0:T(1024)}, u32[]{:S(2)}) copy-start(s32[2048]{0:T(1024)} %pad_clamp_fusion) | copy-start | bytes 24580
  502.5 5.4 copy-start.33
  507.6 0.9 copy-start.6
  511.7 18.6 %copy-start.1 = (f32[1,6,3,96,512]{4,3,2,1,0:T(8,128)S(1)}, f32[1,6,3,96,512]{4,3,2,1,0:T(8,128)}, u32[]{:S(2)}) copy-start(f32[1,6,3,96,512]{4,3,2,1,0:T(8,128)} %param.34) | copy-start | bytes 10616836
  514.2 34.1 %all-to-all-start.1 = ((f32[32,17,288]{2,1,0:T(8,128)}), f32[32,17,288]{2,1,0:T(8,128)}, u32[]{:S(2)}, u32[]{:S(2)}) async-start(f32[32,17,288]{2,1,0:T(8,128)} %all_to_all.19), calls=%async_computation.1 | async-start | bytes 2359296 | tf_op jit(solution)/shard_map/all_to_all | solution.py:121
  518.0 179.8 %all-gather.24.cloned.1.call-start = ((), (), s32[]{:S(2)}) async-start(), calls=%async_computation.8 | async-start | bytes 14155776 | tf_op jit(solution)/shard_map/all_gather | solution.py:140
  530.4 19.3 %copy-start.34 = (s32[1024]{0:T(1024)S(1)}, s32[1024]{0:T(1024)}, u32[]{:S(2)}) copy-start(s32[1024]{0:T(1024)} %pad_clamp_fusion.1) | copy-start | bytes 12292
  552.0 3.5 copy-start.4
  555.5 3.2 copy-start.7
  558.6 0.8 copy-start.12
  558.6 10.5 %copy-start.36 = (f32[1,1,512]{2,1,0:T(1,128)S(1)}, f32[1,1,512]{2,1,0:T(1,128)}, u32[]{:S(2)}) copy-start(f32[1,1,512]{2,1,0:T(1,128)} %get-tuple-element.43) | copy-start | bytes 6148
  559.5 11.5 %copy-start.40 = (f32[96]{0:T(128)S(1)}, f32[96]{0:T(128)}, u32[]{:S(2)}) copy-start(f32[96]{0:T(128)} %multiply_select_fusion) | copy-start | bytes 1156
  583.3 155.1 %all-gather.16.cloned.1.call-start = ((), (), s32[]{:S(2)}) async-start(), calls=%async_computation.4 | async-start | bytes 1769472 | tf_op jit(solution)/shard_map/all_gather | solution.py:38
  714.8 25.5 %copy-start.29 = (s32[2048]{0:T(1024)S(1)}, s32[2048]{0:T(1024)}, u32[]{:S(2)}) copy-start(s32[2048]{0:T(1024)} %pad_clamp_fusion) | copy-start | bytes 24580
  740.3 5.4 copy-start.8
  740.3 5.4 copy-start.13
  740.3 5.4 copy-start.35
Sparse Core Ops, SparseCore 0:
  9.6 31.8 all-gather.17
  93.5 116.0 all-gather.19
  229.3 23.4 all-gather.11
  345.6 114.3 all-gather.21
  477.1 23.4 all-gather.13
  583.4 114.3 all-gather.23
  714.9 23.4 all-gather.15
